TPU v7x, 512 devices: a 8x2x16 block of a 8x8x16 slice. The times are simulated.
512 devices in a mesh: groups: 2 (over y), ep: 128 (over z, x), role: 2 (over core).
Axes of the slice: x: 8, y: 2, z: 16, core: 2. Of those that a mesh axis runs over, the one named last changes fastest.
The devices are a block of a 8x8x16 slice.
Arguments:
- residual: bfloat16 [3072, 2880], P(('groups', 'ep', 'role')), parts along dimension 0, may hold values from -1.796875 to 1.796875
- queries: bfloat16 [3072, 2880], P(('groups', 'ep', 'role')), parts along dimension 0, may hold values from -150 to 150
- key_new: bfloat16 [3072, 320], P(('groups', 'ep', 'role')), parts along dimension 0, may hold values from -6 to 6
- value_new: bfloat16 [3072, 320], P(('groups', 'ep', 'role')), parts along dimension 0, may hold values from -6 to 6
- key_cache: bfloat16 [3072, 128, 320], P(('groups', 'ep', 'role')), parts along dimension 0, may hold values from -6 to 6
- value_cache: bfloat16 [3072, 128, 320], P(('groups', 'ep', 'role')), parts along dimension 0, may hold values from -6 to 6
- lengths: int32 [3072], P(('groups', 'ep', 'role')), parts along dimension 0, may hold values from 1 to 512
- sink_logits: float32 [45], replicated, may hold values from -6 to 6
- norm_gain: float32 [2880], replicated, may hold values from 0.1 to 1.9
- route_ids: int32 [3072, 4], P(('groups', 'ep')), parts along dimension 0, may hold values from 0 to 63, all different within a row; in each aligned block of 12 rows (0 to 11, 12 to 23, ...) at most 2 rows name the same one
- route_logits: float32 [3072, 4], P(('groups', 'ep')), parts along dimension 0, may hold values from -1 to 1
- up_weight: bfloat16 [2880, 92160], P(None, ('ep', 'role')), may hold values from -0.109375 to 0.109375
- down_weight: bfloat16 [92160, 2880], P(('ep', 'role')), may hold values from -0.15625 to 0.15625
Outputs:
- layer_out: bfloat16 [3072, 2880], P(('groups', 'ep', 'role')), parts along dimension 0
There are 2 independent parts, one for each index of `groups`. A program takes and returns all parts, laid end to end along the dimension named above; an argument that names none is the same for every part. Nothing has to cross between parts.
Inputs may be any that keep to these rules, and one draw needn't show every extreme that they name: `route_ids`: in each aligned block of 12 rows (the tokens of one index of ep) no expert is named more than 2 times, a bound that some block reaches.
All inputs are finite; a program needn't handle non-finite values.
Results may differ from a plain program's by a relative error of at most 0.0095.
Values may be sent and summed in bfloat16 or wider, within the bound.
A program may use at most 64 MiB of HBM per device.

v0:
```python
import jax
import jax.numpy as jnp
from jax import lax
from jax.sharding import PartitionSpec as P

HD = 64


def copy_for_each(value, axis):
    copies = jnp.broadcast_to(value, (lax.axis_size(axis), *value.shape))
    return lax.all_to_all(copies, axis, split_axis=0, concat_axis=0, tiled=True)


def joined_along(pieces, dim):
    dims = list(pieces.shape[1:])
    dims[dim] *= pieces.shape[0]
    return jnp.moveaxis(pieces, 0, dim).reshape(dims)


def gathered_copies(value, axis, dim):
    pieces = copy_for_each(value, axis)
    return joined_along(pieces, dim)


def split_up(value, dim, length):
    dims = value.shape
    pieces = value.reshape(*dims[:dim], length, dims[dim] // length, *dims[dim + 1 :])
    return jnp.moveaxis(pieces, dim, 0)


def summed_on_arrival(value, axis, dim):
    length = lax.axis_size(axis)
    pieces = lax.all_to_all(split_up(value, dim, length), axis, 0, 0, tiled=True)
    return jnp.sum(pieces.astype(jnp.float32), axis=0)


def attention(queries, key_new, value_new, key_cache, value_cache, lengths, sink_logits):
    request_count = queries.shape[0]
    window = key_cache.shape[1]
    heads_kv = key_new.shape[1] // HD
    group_size = queries.shape[1] // (heads_kv * HD)
    query_heads = queries.reshape(request_count, heads_kv, group_size, HD)
    cached_keys = key_cache.reshape(request_count, window, heads_kv, HD)
    cached_values = value_cache.reshape(request_count, window, heads_kv, HD)
    fresh_key = key_new.reshape(request_count, heads_kv, HD)
    fresh_value = value_new.reshape(request_count, heads_kv, HD)
    score_scale = HD ** (-0.5)
    cached = (
        jnp.einsum("tkgd,tskd->tkgs", query_heads, cached_keys, preferred_element_type=jnp.float32)
        * score_scale
    )
    fresh_score = (
        jnp.einsum("tkgd,tkd->tkg", query_heads, fresh_key, preferred_element_type=jnp.float32)
        * score_scale
    )
    newest = lengths[:, None] - 1
    slot_index = jnp.arange(window, dtype=jnp.int32)[None, :]
    position = newest - jnp.mod(newest - slot_index, window)
    visible = (position >= 0) & (position >= lengths[:, None] - window + 1)
    cached = jnp.where(visible[:, None, None, :], cached, -1e30)
    sink_logit = sink_logits.reshape(1, heads_kv, group_size)
    highest = jnp.maximum(jnp.maximum(jnp.max(cached, -1), fresh_score), sink_logit)
    weights = jnp.exp(cached - highest[..., None])
    fresh_weight = jnp.exp(fresh_score - highest)
    denominator = jnp.sum(weights, -1) + fresh_weight + jnp.exp(sink_logit - highest)
    cache_probs = (weights / denominator[..., None]).astype(jnp.bfloat16)
    fresh_prob = (fresh_weight / denominator).astype(jnp.bfloat16)
    context = jnp.einsum(
        "tkgs,tskd->tkgd", cache_probs, cached_values, preferred_element_type=jnp.float32
    )
    context = (
        context
        + fresh_prob.astype(jnp.float32)[..., None] * fresh_value.astype(jnp.float32)[:, :, None, :]
    )
    return context.reshape(request_count, -1)


def local(
    residual,
    queries,
    key_new,
    value_new,
    key_cache,
    value_cache,
    lengths,
    sink_logits,
    norm_gain,
    route_ids,
    route_logits,
    up_weight,
    down_weight,
):
    context = attention(queries, key_new, value_new, key_cache, value_cache, lengths, sink_logits)
    hidden_state = residual.astype(jnp.float32) + context
    normed = (
        hidden_state
        * lax.rsqrt(jnp.mean(hidden_state * hidden_state, -1, keepdims=True) + 1e-05)
        * norm_gain
    ).astype(jnp.bfloat16)
    gate_weights = jax.nn.softmax(route_logits, axis=-1)
    pair_count, pick_count = route_ids.shape
    rank_count = lax.axis_size("ep")
    experts = rank_count // 2
    capacity = min(pair_count, max(2, (pair_count * pick_count + experts - 1) // experts))
    width = residual.shape[1]
    tok_rows = gathered_copies(normed, "role", 0)
    onehot = (route_ids[..., None] == jnp.arange(experts, dtype=jnp.int32)).astype(jnp.int32)
    flat_hot = onehot.reshape(-1, experts)
    earlier = jnp.cumsum(flat_hot, axis=0) - flat_hot
    slot_number = jnp.sum(earlier * flat_hot, -1).reshape(pair_count, pick_count)
    slot_hot = (slot_number[..., None] == jnp.arange(capacity, dtype=jnp.int32)).astype(jnp.float32)
    selector = (onehot.astype(jnp.float32)[..., :, None] * slot_hot[..., None, :]).reshape(
        pair_count, pick_count, experts * capacity
    )
    dispatch = jnp.sum(selector, 1).astype(jnp.bfloat16)
    mixing = jnp.sum(selector * gate_weights[..., None], 1)
    packed = jnp.einsum("te,td->ed", dispatch, tok_rows, preferred_element_type=jnp.float32).astype(
        jnp.bfloat16
    )
    outgoing = jnp.repeat(packed.reshape(experts, capacity, width), 2, axis=0)
    half_width = width // 2
    half_start = lax.axis_index("role") * half_width
    outgoing_half = lax.dynamic_slice_in_dim(outgoing, half_start, half_width, 2)
    whole_rows = gathered_copies(
        lax.all_to_all(outgoing_half, "ep", split_axis=0, concat_axis=0, tiled=True), "role", 2
    )
    gathered = whole_rows.reshape(-1, width)
    activation = jax.nn.silu(
        jnp.dot(gathered, up_weight, preferred_element_type=jnp.float32)
    ).astype(jnp.bfloat16)
    partial_value = jnp.dot(activation, down_weight, preferred_element_type=jnp.float32).astype(
        jnp.bfloat16
    )
    partial_value = partial_value.reshape(whole_rows.shape[0], whole_rows.shape[1], width).astype(
        jnp.float32
    )
    summed = summed_on_arrival(partial_value.astype(jnp.bfloat16), "role", 2)
    returned_rows = lax.all_to_all(
        summed.astype(jnp.bfloat16), "ep", split_axis=0, concat_axis=0, tiled=True
    ).astype(summed.dtype)
    pair_sum = jnp.sum(returned_rows.reshape(experts, 2, capacity, half_width), 1).reshape(
        experts * capacity, half_width
    )
    mixed = jnp.dot(mixing, pair_sum)
    expert_out = lax.all_to_all(
        mixed.astype(jnp.bfloat16), "role", split_axis=0, concat_axis=1, tiled=True
    ).astype(mixed.dtype)
    return (hidden_state + expert_out).astype(jnp.bfloat16)


def solution(mesh):
    placed = (
        P(("groups", "ep", "role"), None),
        P(("groups", "ep", "role"), None),
        P(("groups", "ep", "role"), None),
        P(("groups", "ep", "role"), None),
        P(("groups", "ep", "role"), None, None),
        P(("groups", "ep", "role"), None, None),
        P(("groups", "ep", "role")),
        P(),
        P(),
        P(("groups", "ep"), None),
        P(("groups", "ep"), None),
        P(None, ("ep", "role")),
        P(("ep", "role"), None),
    )
    return jax.shard_map(
        local,
        mesh=mesh,
        in_specs=placed,
        out_specs=P(("groups", "ep", "role"), None),
        check_vma=False,
    )
```

profile of v0, /device:TPU:65, one launch (start us, length us, event | category | flops | bytes accessed | tf_op | source)
XLA Modules:
  0.0 224.2 jit_solution(6895238387746101604)
XLA Ops:
  0.0 0.8 broadcast_add_fusion.1
  1.5 0.8 reshape.165
  3.1 0.9 reshape.146
  4.3 1.4 fusion.23
  7.4 44.8 %all-to-all-start = ((bf16[2,6,2880]{2,1,0:T(8,128)(2,1)}), bf16[2,6,2880]{2,1,0:T(8,128)(2,1)S(1)}, u32[]{:S(2)}, u32[]{:S(2)}) async-start(bf16[2,6,2880]{2,1,0:T(8,128)(2,1)} %broadcast_in_dim.20), calls=%async_computation | async-start | bytes 188416 | tf_op jit(solution)/shard_map/all_to_all | solution.py:11
  53.9 1.2 copy.77
  55.1 2.1 reshape.152
  58.0 1.6 constant_dynamic-slice_fusion
  59.6 51.0 %all_to_all.38 = bf16[128,2,1440]{2,1,0:T(2,128)(2,1)S(1)} all-to-all(bf16[128,2,1440]{2,1,0:T(2,128)(2,1)S(1)} %constant_dynamic-slice_fusion), channel_id=1, replica_groups=mesh['groups'=2,'ep'=128,'role'=2] {'ep'}, dimensions={0} | all-to-all | bytes 1474560 | tf_op jit(solution)/shard_map/all_to_all | solution.py:125
  110.6 1.8 copy.78
  112.5 1.3 broadcast_in_dim.22
  113.8 9.6 %all_to_all.39 = bf16[2,128,2,1440]{1,3,2,0:T(8,128)(2,1)} all-to-all(bf16[2,128,2,1440]{1,3,2,0:T(8,128)(2,1)S(1)} %broadcast_in_dim.22), channel_id=1, replica_groups=mesh['groups'=2,'ep'=128,'role'=2] {'role'}, dimensions={0} | all-to-all | bytes 2949120 | tf_op jit(solution)/shard_map/all_to_all | solution.py:11
  123.4 5.0 %copy.79 = bf16[128,2,2,1440]{3,2,1,0:T(2,128)(2,1)} copy(bf16[128,2,2,1440]{0,3,1,2:T(8,128)(2,1)} %bitcast.41) | data formatting | bytes 2949120 | tf_op jit(solution)/shard_map/transpose | solution.py:17
  128.4 5.0 %reshape_reshape.3 = bf16[256,2880]{1,0:T(8,128)(2,1)} reshape(bf16[128,2,2,1440]{3,2,1,0:T(2,128)(2,1)} %copy.79) | data formatting | bytes 2949120 | tf_op jit(solution)/shard_map/reshape;reshape | solution.py:127
  133.4 6.0 %convolution_convert_fusion = bf16[256,2880]{0,1:T(8,128)(2,1)} fusion(bf16[360,2880]{1,0:T(8,128)(2,1)S(1)} %copy-done, bf16[256,2880]{1,0:T(8,128)(2,1)} %reshape_reshape.3, bf16[2880,360]{0,1:T(8,128)(2,1)} %param.24), kind=kOutput, calls=%fused_computation | convolution fusion | flops 1062881280 | bytes 7096320 | tf_op jit(solution)/shard_map/dot_general | solution.py:131
  139.4 2.5 %copy.80 = bf16[256,2880]{1,0:T(8,128)(2,1)} copy(bf16[256,2880]{0,1:T(8,128)(2,1)} %convolution_convert_fusion) | data formatting | bytes 2949120 | tf_op jit(solution)/shard_map/convert_element_type | solution.py:131
  141.9 5.8 %reshape.154 = bf16[128,2,2,1440]{3,2,1,0:T(2,128)(2,1)} reshape(bf16[256,2880]{1,0:T(8,128)(2,1)} %copy.80) | data formatting | bytes 2949120 | tf_op jit(solution)/shard_map/reshape | solution.py:27
  147.7 4.9 %copy.81 = bf16[2,128,2,1440]{1,3,2,0:T(8,128)(2,1)} copy(bf16[2,128,2,1440]{3,0,2,1:T(2,128)(2,1)} %bitcast.40) | data formatting | bytes 2949120 | tf_op jit(solution)/shard_map/transpose | solution.py:28
  152.6 7.5 %all_to_all.40 = bf16[2,128,2,1440]{1,3,2,0:T(8,128)(2,1)} all-to-all(bf16[2,128,2,1440]{1,3,2,0:T(8,128)(2,1)} %copy.81), channel_id=1, replica_groups=mesh['groups'=2,'ep'=128,'role'=2] {'role'}, dimensions={0} | all-to-all | bytes 2949120 | tf_op jit(solution)/shard_map/all_to_all | solution.py:33
  160.1 2.7 %reduce_sum.81 = bf16[128,2,1440]{0,2,1:T(8,128)(2,1)} reduce(bf16[2,128,2,1440]{1,3,2,0:T(8,128)(2,1)} %all_to_all.40, bf16[]{:T(256)} %constant.55.clone.1), dimensions={0}, to_apply=%region_9.10 | reduce | flops 368640 | bytes 2211842 | tf_op jit(solution)/shard_map/reduce_sum | solution.py:34
  162.8 2.3 %copy.82 = bf16[128,2,1440]{2,1,0:T(2,128)(2,1)S(1)} copy(bf16[128,2,1440]{0,2,1:T(8,128)(2,1)} %reduce_sum.81) | data formatting | bytes 1474560 | tf_op jit(solution)/shard_map/reduce_sum | solution.py:34
  165.1 49.4 %all_to_all.41 = bf16[128,2,1440]{2,1,0:T(2,128)(2,1)S(1)} all-to-all(bf16[128,2,1440]{2,1,0:T(2,128)(2,1)S(1)} %copy.82), channel_id=1, replica_groups=mesh['groups'=2,'ep'=128,'role'=2] {'ep'}, dimensions={0} | all-to-all | bytes 1474560 | tf_op jit(solution)/shard_map/all_to_all | solution.py:138
  214.5 1.0 convert_reduce_fusion
  215.8 7.6 %all_to_all.42 = bf16[2,6,1440]{2,1,0:T(8,128)(2,1)S(1)} all-to-all(bf16[2,6,1440]{2,1,0:T(8,128)(2,1)S(1)} %all_to_all.30), channel_id=1, replica_groups=mesh['groups'=2,'ep'=128,'role'=2] {'role'}, dimensions={0} | all-to-all | bytes 69120 | tf_op jit(solution)/shard_map/all_to_all | solution.py:145
  (49 shorter events, 6.9 us)
Async XLA Ops:
  0.0 133.4 %copy-start = (bf16[360,2880]{1,0:T(8,128)(2,1)S(1)}, bf16[360,2880]{1,0:T(8,128)(2,1)}, u32[]{:S(2)}) copy-start(bf16[360,2880]{1,0:T(8,128)(2,1)} %param.25) | copy-start | bytes 6220804
  0.0 6.0 %copy-start.5 = (bf16[6,128,320]{1,2,0:T(8,128)(2,1)S(1)}, bf16[6,128,320]{1,2,0:T(8,128)(2,1)}, u32[]{:S(2)}) copy-start(bf16[6,128,320]{1,2,0:T(8,128)(2,1)} %param.18) | copy-start | bytes 1474564
  4.3 2.3 %copy-start.1 = (bf16[6,2880]{1,0:T(8,128)(2,1)S(1)}, bf16[6,2880]{1,0:T(8,128)(2,1)}, u32[]{:S(2)}) copy-start(bf16[6,2880]{1,0:T(8,128)(2,1)} %param.13) | copy-start | bytes 103684
  5.7 1.1 copy-start.3
  5.7 46.5 %copy-start.4 = (s32[12,4]{0,1:T(4,128)S(1)}, s32[12,4]{0,1:T(4,128)}, u32[]{:S(2)}) copy-start(s32[12,4]{0,1:T(4,128)} %param.22) | copy-start | bytes 580
  5.7 46.8 %copy-start.2 = (f32[12,4]{0,1:T(4,128)S(1)}, f32[12,4]{0,1:T(4,128)}, u32[]{:S(2)}) copy-start(f32[12,4]{0,1:T(4,128)} %param.23) | copy-start | bytes 580
  7.4 45.9 %all-to-all-start = ((bf16[2,6,2880]{2,1,0:T(8,128)(2,1)}), bf16[2,6,2880]{2,1,0:T(8,128)(2,1)S(1)}, u32[]{:S(2)}, u32[]{:S(2)}) async-start(bf16[2,6,2880]{2,1,0:T(8,128)(2,1)} %broadcast_in_dim.20), calls=%async_computation | async-start | bytes 188416 | tf_op jit(solution)/shard_map/all_to_all | solution.py:11
where the time goes:
time: 225 us; the launch traced here: 224 us
  blocking collectives  125 us (56%)
  starting transfers between devices  44.8 us (20%)
  local copies, waits for them, and re-layouts  39.1 us (17%)
  matrix products  8.62 us (4%)
  other arithmetic  6.44 us (3%)
    all_to_all x1, blocking collectives, local(): lax.all_to_all(outgoing_half, 'ep', split_axis=0, concat_axis=0, tiled=True)  51 us
    all_to_all x1, blocking collectives, local(): lax.all_to_all(summed.astype(jnp.bfloat16), 'ep', split_axis=0, concat_ax...  49.4 us
    all_to_all x1, starting transfers between devices, copy_for_each(): return lax.all_to_all(copies, axis, split_axis=0, concat_axis=0, tiled=True)  44.8 us
    all_to_all x1, blocking collectives, copy_for_each(): return lax.all_to_all(copies, axis, split_axis=0, concat_axis=0, tiled=True)  9.56 us
    all_to_all x1, blocking collectives, local(): lax.all_to_all(mixed.astype(jnp.bfloat16), 'role', split_axis=0, concat_a...  7.56 us
    all_to_all x1, blocking collectives, summed_on_arrival(): lax.all_to_all(split_up(value, dim, length), axis, 0, 0, tiled=True)  7.49 us
    dot_general x1, matrix products, local(): jnp.dot(activation, down_weight, preferred_element_type=jnp.float32)  6.01 us
    reshape x1, local copies, waits for them, and re-layouts, split_up(): value.reshape(*dims[:dim], length, dims[dim] // length, *dims[dim + 1:])  5.78 us
  transfers between devices with their start and end apart: 1, of which 0 were waited for; matrix products, arithmetic and copies ran while one was open for 1% of the time, Pallas kernels for 0%

commit v1 on v0

v1 whole, which is shorter than its diff:
```python
import functools

import jax
import jax.numpy as jnp
from jax import lax
from jax.experimental import pallas as pl
from jax.experimental.pallas import tpu as pltpu
from jax.sharding import PartitionSpec as P

HD = 64
ROWS = 8
TILE = 16
MESH = pl.DeviceIdType.MESH
BF16 = jnp.bfloat16
F32 = jnp.float32


def attention(queries, key_new, value_new, key_cache, value_cache, lengths, sink_logits):
    request_count = queries.shape[0]
    window = key_cache.shape[1]
    heads_kv = key_new.shape[1] // HD
    group_size = queries.shape[1] // (heads_kv * HD)
    query_heads = queries.reshape(request_count, heads_kv, group_size, HD)
    cached_keys = key_cache.reshape(request_count, window, heads_kv, HD)
    cached_values = value_cache.reshape(request_count, window, heads_kv, HD)
    fresh_key = key_new.reshape(request_count, heads_kv, HD)
    fresh_value = value_new.reshape(request_count, heads_kv, HD)
    score_scale = HD ** (-0.5)
    cached = (
        jnp.einsum("tkgd,tskd->tkgs", query_heads, cached_keys, preferred_element_type=jnp.float32)
        * score_scale
    )
    fresh_score = (
        jnp.einsum("tkgd,tkd->tkg", query_heads, fresh_key, preferred_element_type=jnp.float32)
        * score_scale
    )
    newest = lengths[:, None] - 1
    slot_index = jnp.arange(window, dtype=jnp.int32)[None, :]
    position = newest - jnp.mod(newest - slot_index, window)
    visible = (position >= 0) & (position >= lengths[:, None] - window + 1)
    cached = jnp.where(visible[:, None, None, :], cached, -1e30)
    sink_logit = sink_logits.reshape(1, heads_kv, group_size)
    highest = jnp.maximum(jnp.maximum(jnp.max(cached, -1), fresh_score), sink_logit)
    weights = jnp.exp(cached - highest[..., None])
    fresh_weight = jnp.exp(fresh_score - highest)
    denominator = jnp.sum(weights, -1) + fresh_weight + jnp.exp(sink_logit - highest)
    cache_probs = (weights / denominator[..., None]).astype(jnp.bfloat16)
    fresh_prob = (fresh_weight / denominator).astype(jnp.bfloat16)
    context = jnp.einsum(
        "tkgs,tskd->tkgd", cache_probs, cached_values, preferred_element_type=jnp.float32
    )
    context = (
        context
        + fresh_prob.astype(jnp.float32)[..., None] * fresh_value.astype(jnp.float32)[:, :, None, :]
    )
    return context.reshape(request_count, -1)


def ring_offsets(n):
    offsets = [0]
    for d in range(1, n // 2 + 1):
        offsets += [d] if 2 * d == n else [d, -d]
    opposite = [next(b for b, o in enumerate(offsets) if (o + offsets[a]) % n == 0) for a in range(n)]
    return offsets, opposite


def moe_kernel(
    nx, nz, capacity, width, chunk,
    normed, table, up_hbm, down_hbm, out,
    up, down, gath, tabs, packed, rows, part, part_in, half_out, half_in, back, returned, mixed, final,
    weight_sem, tab_s, tab_r, gath_s, gath_r, out_s, out_r, fwd_s, fwd_r, back_s, back_r, fin_s, fin_r,
):
    ep, role = lax.axis_index("ep"), lax.axis_index("role")
    z, x = ep // nx, ep % nx
    half = x % 2
    mine = x * 2 + role
    quarter = half * 2 + role
    sibling = {"ep": ep, "role": 1 - role}
    pair = {"ep": ep + 1 - 2 * half, "role": role}
    qw = packed.shape[-1]
    block = nx * capacity
    offsets, opposite = ring_offsets(nz)
    plane = [(d, f) for d in range(nx) for f in range(2) if d or f]

    def in_plane(d, f):
        other_x, other_role = (x + d) % nx, (role + f) % 2
        return other_x, other_role, {"ep": z * nx + other_x, "role": other_role}

    def along_z(k):
        return {"ep": ((z + offsets[k] + nz) % nz) * nx + x, "role": role}

    def send(src, dst, ssem, rsem, device):
        copy = pltpu.make_async_remote_copy(
            src_ref=src, dst_ref=dst, send_sem=ssem, recv_sem=rsem, device_id=device, device_id_type=MESH
        )
        copy.start()
        return copy

    sent = []
    barrier = pltpu.get_barrier_semaphore()
    for d, f in plane:
        pl.semaphore_signal(barrier, inc=1, device_id=in_plane(d, f)[2], device_id_type=MESH)
    for k in range(1, nz):
        pl.semaphore_signal(barrier, inc=1, device_id=along_z(k), device_id_type=MESH)
    up_copy = pltpu.make_async_copy(up_hbm, up.at[pl.ds(0, width), :], weight_sem.at[0])
    up_copy.start()
    down_copy = pltpu.make_async_copy(down_hbm, down, weight_sem.at[1])
    down_copy.start()
    pl.semaphore_wait(barrier, len(plane) + nz - 1)

    tab_copies, gath_copies = [], []
    for n, (d, f) in enumerate(plane):
        other_x, other_role, device = in_plane(d, f)
        if f == 0:
            tab_copies.append(send(table.at[other_x // 2], tabs.at[x], tab_s.at[d], tab_r.at[d], device))
        wanted = (other_x % 2) * 2 + other_role
        gath_copies.append(send(normed.at[wanted], gath.at[mine], gath_s.at[n], gath_r.at[n], device))
    up[pl.ds(width, 4 * qw - width), :] = jnp.zeros((4 * qw - width, up.shape[1]), BF16)
    gath[mine] = normed[quarter]
    tabs[x] = table[x // 2]
    last = width - 3 * qw
    clear = last // 128 * 128
    for h in (1,):
        part[h, 1, :, :, clear:] = jnp.zeros((nz, block, qw - clear), BF16)
    for copy in tab_copies:
        copy.wait_recv()
    lanes = tabs.shape[-1] // 2
    codes = jnp.sum(tabs[...].astype(F32), axis=0)
    slots, gates = codes[:, :lanes], codes[:, lanes:]
    row = lax.broadcasted_iota(jnp.int32, (nz, block, lanes), 1)
    col = lax.broadcasted_iota(jnp.int32, (nz, block, lanes), 2)
    hit = (col // (2 * ROWS) == row // capacity) & (
        jnp.broadcast_to(slots[:, None, :], (nz, block, lanes)) == (row % capacity + 1).astype(F32)
    )
    choose = jnp.where(hit, 1.0, 0.0).astype(BF16).reshape(nz * block, lanes)
    blend = jnp.where(hit, jnp.broadcast_to(gates[:, None, :], (nz, block, lanes)), 0.0).astype(BF16)
    blend = blend.reshape(nz * block, lanes)
    for copy in gath_copies:
        copy.wait_recv()
    tokens = gath[...].reshape(2 * nx * ROWS, qw)
    if tokens.shape[0] < lanes:
        tokens = jnp.concatenate([tokens, jnp.zeros((lanes - tokens.shape[0], qw), BF16)], axis=0)
    packed[...] = jnp.dot(choose, tokens, preferred_element_type=F32).astype(BF16).reshape(nz, block, qw)

    out_copies = {}
    for k in range(1, nz):
        to = opposite[k]
        out_copies[k] = send(packed.at[k], rows.at[quarter, to], out_s.at[k], out_r.at[to], along_z(k))
    rows[quarter, 0] = packed[0]
    back_copies = {}
    live = {}
    chunks = nz // chunk

    def span(c):
        return pl.ds(c * chunk, chunk)

    def stage_in(c):
        for k in range(c * chunk, (c + 1) * chunk):
            if k:
                out_copies[opposite[k]].wait_recv()
        mine_rows = rows.at[quarter, span(c)]
        live["pair", c] = send(mine_rows, mine_rows, fwd_s.at[0, c], fwd_r.at[0, c], pair)
        live["sib", c] = send(mine_rows, mine_rows, fwd_s.at[1, c], fwd_r.at[1, c], sibling)

    def stage_relay(c):
        live["pair", c].wait_recv()
        their_rows = rows.at[(1 - half) * 2 + role, span(c)]
        live["relay", c] = send(their_rows, their_rows, fwd_s.at[2, c], fwd_r.at[2, c], sibling)

    def stage_ffn(c):
        live["sib", c].wait_recv()
        live["relay", c].wait_recv()
        if c == 0:
            up_copy.wait()
        total = None
        for q in range(4):
            piece = rows[q, c * chunk : (c + 1) * chunk].reshape(chunk * block, qw)
            term = jnp.dot(piece, up[q * qw : (q + 1) * qw, :], preferred_element_type=F32)
            total = term if total is None else total + term
        active = (total / (1.0 + jnp.exp(-total))).astype(BF16)
        if c == 0:
            down_copy.wait()
        for q in range(4):
            w = min(qw, width - q * qw)
            value = jnp.dot(active, down[:, q * qw : q * qw + w], preferred_element_type=F32).astype(BF16)
            part[q // 2, q % 2, c * chunk : (c + 1) * chunk, :, :w] = value.reshape(chunk, block, w)
        live["part", c] = send(
            part.at[:, 1 - role, span(c)], part_in.at[:, span(c)], fwd_s.at[3, c], fwd_r.at[3, c], sibling
        )

    def stage_half(c):
        live["part", c].wait_recv()
        at = slice(c * chunk, (c + 1) * chunk)
        half_out[at] = (part[1 - half, role, at].astype(F32) + part_in[1 - half, at].astype(F32)).astype(BF16)
        live["half", c] = send(half_out.at[span(c)], half_in.at[span(c)], fwd_s.at[4, c], fwd_r.at[4, c], pair)

    def stage_back(c):
        live["half", c].wait_recv()
        at = slice(c * chunk, (c + 1) * chunk)
        back[at] = (
            part[half, role, at].astype(F32) + part_in[half, at].astype(F32) + half_in[at].astype(F32)
        ).astype(BF16)
        for k in range(c * chunk, (c + 1) * chunk):
            if k == 0:
                returned[0] = back[0]
            else:
                to = opposite[k]
                back_copies[k] = send(back.at[k], returned.at[to], back_s.at[k], back_r.at[to], along_z(k))

    for t in range(chunks + 2):
        if t < chunks:
            stage_in(t)
        if 0 <= t - 1 < chunks:
            stage_relay(t - 1)
            stage_ffn(t - 1)
            stage_half(t - 1)
        if 0 <= t - 2 < chunks:
            stage_back(t - 2)

    for k in range(1, nz):
        back_copies[opposite[k]].wait_recv()
    mix = lax.dot_general(
        blend, returned[...].reshape(nz * block, qw), (((0,), (0,)), ((), ())), preferred_element_type=F32
    )
    mixed[...] = mix[: 2 * nx * ROWS].astype(BF16).reshape(2 * nx, ROWS, qw)
    fin_copies = []
    for n, (d, f) in enumerate(plane):
        other_x, other_role, device = in_plane(d, f)
        fin_copies.append(
            send(mixed.at[other_x * 2 + other_role], final.at[mine], fin_s.at[n], fin_r.at[n], device)
        )
    final[mine] = mixed[mine]
    for copy in fin_copies:
        copy.wait_recv()
    for q in range(4):
        total = None
        for p in range(nx // 2):
            term = final[(2 * p + q // 2) * 2 + q % 2].astype(F32)
            total = term if total is None else total + term
        out[:, q * qw : (q + 1) * qw] = total
    for copy in (
        tab_copies + gath_copies + list(out_copies.values()) + list(live.values())
        + list(back_copies.values()) + fin_copies
    ):
        copy.wait_send()


def experts_of_tokens(normed, table, up_weight, down_weight, nx, nz, capacity, width):
    qw = normed.shape[-1]
    hidden = up_weight.shape[1]
    block = nx * capacity
    chunk = max(1, nz // 4)
    chunks = nz // chunk
    any_space = pl.BlockSpec(memory_space=pl.ANY)
    vmem = pl.BlockSpec(memory_space=pltpu.VMEM)
    dma = pltpu.SemaphoreType.DMA
    return pl.pallas_call(
        functools.partial(moe_kernel, nx, nz, capacity, width, chunk),
        out_shape=jax.ShapeDtypeStruct((ROWS, 4 * qw), F32),
        in_specs=[vmem, vmem, any_space, any_space],
        out_specs=vmem,
        scratch_shapes=[
            pltpu.VMEM((4 * qw, hidden), BF16),
            pltpu.VMEM((hidden, width), BF16),
            pltpu.VMEM((2 * nx, ROWS, qw), BF16),
            pltpu.VMEM((nx, *table.shape[1:]), BF16),
            pltpu.VMEM((nz, block, qw), BF16),
            pltpu.VMEM((4, nz, block, qw), BF16),
            pltpu.VMEM((2, 2, nz, block, qw), BF16),
            pltpu.VMEM((2, nz, block, qw), BF16),
            pltpu.VMEM((nz, block, qw), BF16),
            pltpu.VMEM((nz, block, qw), BF16),
            pltpu.VMEM((nz, block, qw), BF16),
            pltpu.VMEM((nz, block, qw), BF16),
            pltpu.VMEM((2 * nx, ROWS, qw), BF16),
            pltpu.VMEM((2 * nx, ROWS, qw), BF16),
            dma((2,)),
            dma((nx,)), dma((nx,)),
            dma((2 * nx,)), dma((2 * nx,)),
            dma((nz,)), dma((nz,)),
            dma((5, chunks)), dma((5, chunks)),
            dma((nz,)), dma((nz,)),
            dma((2 * nx,)), dma((2 * nx,)),
        ],
        compiler_params=pltpu.CompilerParams(collective_id=0, has_side_effects=True),
        name="experts_of_tokens",
    )(normed, table, up_weight, down_weight)


def slot_tables(route_ids, gate_weights, capacity, nx, nz, lanes):
    pair_count, pick_count = route_ids.shape
    ep = lax.axis_index("ep")
    z, x = ep // nx, ep % nx
    flat = route_ids.reshape(-1)
    count = flat.shape[0]
    index = jnp.arange(count, dtype=jnp.int32)
    same = (flat[:, None] == flat[None, :]) & (index[None, :] < index[:, None])
    slot = jnp.sum(same.astype(jnp.int32), -1)
    offsets, _ = ring_offsets(nz)
    planes = (z + jnp.array(offsets, jnp.int32) + nz) % nz
    experts = (planes[None, :] * (nx // 2) + jnp.arange(nx // 2, dtype=jnp.int32)[:, None]).reshape(-1)
    named = (experts[:, None] == flat[None, :]).astype(F32)
    token = index // pick_count
    per_device = pair_count // 2
    column = x * 2 * ROWS + token // per_device * ROWS + token % per_device
    here = column[:, None] == jnp.arange(lanes, dtype=jnp.int32)[None, :]
    values = jnp.concatenate(
        [
            jnp.where(here, (slot + 1).astype(F32)[:, None], 0.0),
            jnp.where(here, gate_weights.reshape(-1)[:, None], 0.0),
        ],
        axis=1,
    )
    return jnp.dot(named, values).astype(BF16).reshape(nx // 2, nz, 2 * lanes)


def local(
    residual,
    queries,
    key_new,
    value_new,
    key_cache,
    value_cache,
    lengths,
    sink_logits,
    norm_gain,
    route_ids,
    route_logits,
    up_weight,
    down_weight,
):
    context = attention(queries, key_new, value_new, key_cache, value_cache, lengths, sink_logits)
    hidden_state = residual.astype(F32) + context
    normed = (
        hidden_state
        * lax.rsqrt(jnp.mean(hidden_state * hidden_state, -1, keepdims=True) + 1e-05)
        * norm_gain
    ).astype(BF16)
    gate_weights = jax.nn.softmax(route_logits, axis=-1)
    pair_count, pick_count = route_ids.shape
    rank_count = lax.axis_size("ep")
    experts = rank_count // 2
    capacity = min(pair_count, max(2, (pair_count * pick_count + experts - 1) // experts))
    nx = TILE // capacity
    nz = rank_count // nx
    count, width = residual.shape
    qw = -(-width // (4 * 128)) * 128
    lanes = -(-2 * nx * ROWS // 128) * 128
    table = slot_tables(route_ids, gate_weights, capacity, nx, nz, lanes)
    normed = jnp.pad(normed, ((0, ROWS - count), (0, 4 * qw - width)))
    normed = normed.reshape(ROWS, 4, qw).transpose(1, 0, 2)
    expert_out = experts_of_tokens(normed, table, up_weight, down_weight, nx, nz, capacity, width)
    return (hidden_state + expert_out[:count, :width]).astype(BF16)


def solution(mesh):
    placed = (
        P(("groups", "ep", "role"), None),
        P(("groups", "ep", "role"), None),
        P(("groups", "ep", "role"), None),
        P(("groups", "ep", "role"), None),
        P(("groups", "ep", "role"), None, None),
        P(("groups", "ep", "role"), None, None),
        P(("groups", "ep", "role")),
        P(),
        P(),
        P(("groups", "ep"), None),
        P(("groups", "ep"), None),
        P(None, ("ep", "role")),
        P(("ep", "role"), None),
    )
    return jax.shard_map(
        local,
        mesh=mesh,
        in_specs=placed,
        out_specs=P(("groups", "ep", "role"), None),
        check_vma=False,
    )
```

time: 225 us -> 132 us (0.59)
  blocking collectives: 125 us -> 0 us
  Pallas kernels: 0 us -> 114 us
  starting transfers between devices: 44.8 us -> 0 us
  local copies, waits for them, and re-layouts: 39.1 us -> 8.68 us
  matrix products: 8.62 us -> 2.77 us
    all_to_all x5 -> x0, blocking collectives: 125 us -> none  [the longest x1 51 us: local(): lax.all_to_all(outgoing_half, 'ep', split_axis=0, concat_axis=0, tiled=True)]
    pallas_call x0 -> x1, Pallas kernels: none -> 114 us  [experts_of_tokens(): pl.pallas_call(functools.partial(moe_kernel, nx, nz, capacity, width, chu...]
    all_to_all x1 -> x0, starting transfers between devices: 44.8 us -> none  [copy_for_each(): return lax.all_to_all(copies, axis, split_axis=0, concat_axis=0, tiled=True)]
    transpose x2 -> x0, local copies, waits for them, and re-layouts: 9.9 us -> none  [the longest x1 5.02 us: joined_along(): return jnp.moveaxis(pieces, 0, dim).reshape(dims)]
    reshape x3 -> x0, local copies, waits for them, and re-layouts: 7.95 us -> none  [the longest x1 5.78 us: split_up(): value.reshape(*dims[:dim], length, dims[dim] // length, *dims[dim + 1:])]
    dot_general x3 -> x1, matrix products: 6.64 us -> 0.81 us  [slot_tables(): return jnp.dot(named, values).astype(BF16).reshape(nx // 2, nz, 2 * lanes)]
    another operation x1 -> x0, local copies, waits for them, and re-layouts: 5.01 us -> none  [local(): gathered = whole_rows.reshape(-1, width)]
    unnamed x13 -> x10, local copies, waits for them, and re-layouts: 0.12 us -> 4.38 us
  transfers between devices with their start and end apart: 1 -> 0, of which waited for: 0 -> 0; matrix products, arithmetic and copies ran while one was open for 1% -> 0% of each run, Pallas kernels for 0% -> 0%
where the time goes in v1:
time: 132 us; the launch traced here: 131 us
  Pallas kernels  114 us (86%)
  local copies, waits for them, and re-layouts  8.68 us (7%)
  other arithmetic  5.85 us (4%)
  matrix products  2.77 us (2%)
    pallas_call x1, Pallas kernels, experts_of_tokens(): pl.pallas_call(functools.partial(moe_kernel, nx, nz, capacity, width, chu...  114 us
    unnamed x10, local copies, waits for them, and re-layouts  4.38 us

profile of v1, /device:TPU:65, one launch (start us, length us, event | category | flops | bytes accessed | tf_op | source)
XLA Modules:
  0.0 131.0 jit_solution(8932123653976367704)
XLA Ops:
  0.0 1.0 copy-done
  1.0 0.7 fusion.26
  1.7 0.7 reduce_max.19
  2.4 0.7 fusion.24
  3.1 0.7 fusion.23
  3.8 0.7 broadcast_add_fusion.1
  4.7 0.1 broadcast_in_dim.55
  4.8 0.7 max.15
  5.6 0.8 copy.21
  6.4 0.2 convert_reduce_fusion
  6.6 0.8 reshape.162
  7.5 0.8 convolution_convert_fusion
  8.3 0.8 reshape.158
  9.1 0.9 reshape.151
  10.0 0.2 fusion.30
  10.2 0.3 fusion.29
  10.5 0.3 fusion.1
  10.8 1.5 %convolution_add_fusion = f32[6,5,9,64]{3,2,1,0:T(8,128)S(1)} fusion(bf16[6,128,5,64]{1,3,2,0:T(8,128)(2,1)} %bitcast.29, f32[6,5,9,128]{3,2,1,0:T(8,128)S(1)} %get-tuple-element.12, f32[6,5,64]{2,1,0:T(8,128)S(1)} %reshape.158, f32[6,5,9]{2,1,0:T(8,128)S(1)} %get-tuple-element.5, f32[6,5,9]{2,1,0:T(8,128)S(1)} %get-tuple-element.6, f32[6,5,9]{2,1,0:T(8,128)S(1)} %fusion.10), kind=kOutput, calls=%fused_computation | convolution fusion | flops 4561920 | bytes 709800 | tf_op jit(solution)/shard_map/tkgs,tskd->tkgd/dot_general | solution.py:49
  12.3 0.1 reshape.155
  12.4 0.1 multiply_reduce_fusion
  12.7 0.6 pad.4
  13.3 2.6 %copy.23.up_hbm = bf16[2880,360]{1,0:T(8,128)(2,1)} copy(bf16[2880,360]{0,1:T(8,128)(2,1)S(1)} %copy-done.1) | data formatting | bytes 4147200 | tf_op args[11]
  15.9 113.6 %experts_of_tokens.1 = f32[8,3072]{1,0:T(8,128)} custom-call(bf16[4,8,768]{2,1,0:T(8,128)(2,1)} %bitcast.27, bf16[4,16,256]{2,1,0:T(8,128)(2,1)} %bitcast.28, bf16[2880,360]{1,0:T(8,128)(2,1)} %copy.23.up_hbm, bf16[360,2880]{1,0:T(8,128)(2,1)} %down_hbm.1), custom_call_target="tpu_custom_call" | custom-call | tf_op jit(solution)/shard_map/experts_of_tokens/pallas_call | solution.py:257
  129.5 1.5 %add_convert_fusion = bf16[6,2880]{1,0:T(8,128)(2,1)} fusion(f32[8,3072]{1,0:T(8,128)} %experts_of_tokens.1, f32[6,2880]{1,0:T(8,128)S(1)} %reshape.155, bf16[6,2880]{1,0:T(8,128)(2,1)S(1)} %copy-done.2), kind=kLoop, calls=%fused_computation.9 | loop fusion | flops 69120 | bytes 207360 | tf_op jit(solution)/shard_map/convert_element_type | solution.py:353
  (18 shorter events, 0.6 us)
Async XLA Ops:
  0.0 1.0 copy-start
  0.0 12.4 %copy-start.2 = (bf16[6,2880]{1,0:T(8,128)(2,1)S(1)}, bf16[6,2880]{1,0:T(8,128)(2,1)}, u32[]{:S(2)}) copy-start(bf16[6,2880]{1,0:T(8,128)(2,1)} %param.14) | copy-start | bytes 103684
  0.0 12.6 %copy-start.3 = (f32[2880]{0:T(1024)S(1)}, f32[2880]{0:T(1024)}, u32[]{:S(2)}) copy-start(f32[2880]{0:T(1024)} %param.22) | copy-start | bytes 34564
  7.5 5.8 %copy-start.1 = (bf16[2880,360]{0,1:T(8,128)(2,1)S(1)}, bf16[2880,360]{0,1:T(8,128)(2,1)}, u32[]{:S(2)}) copy-start(bf16[2880,360]{0,1:T(8,128)(2,1)} %param.25) | copy-start | bytes 6220804

commit v2 on v1

v2 whole, which is shorter than its diff:
```python
import functools

import jax
import jax.numpy as jnp
from jax import lax
from jax.experimental import pallas as pl
from jax.experimental.pallas import tpu as pltpu
from jax.sharding import PartitionSpec as P

HD = 64
ROWS = 8
TILE = 16
ORDER = "i0 r0 f0 i1 h0 r1 f1 b0 i2 h1 r2 f2 b1 i3 h2 r3 f3 b2 h3 b3"
CHUNKS = [4, 4, 4, 4]
MESH = pl.DeviceIdType.MESH
BF16 = jnp.bfloat16
F32 = jnp.float32


def ring_offsets(n):
    offsets = []
    for d in range(n // 2, 0, -1):
        offsets += [d] if 2 * d == n else [-d, d]
    offsets.append(0)
    opposite = [next(b for b, o in enumerate(offsets) if (o + offsets[a]) % n == 0) for a in range(n)]
    return offsets, opposite


def layer_kernel(
    nx, nz, capacity, picks, chunks, order,
    lengths, residual_hbm, queries_hbm, key_new_hbm, value_new_hbm, key_hbm, value_hbm, sink_hbm, gain_hbm,
    ids_hbm, logits_hbm, up_hbm, down_hbm, out,
    residual_v, queries_v, key_new, value_new, keys, values, sink_v, gain, ids_v, logits_v,
    wide, by_group, by_token, hidden, lanes_v, normed, table,
    up, down, gath, tabs, packed, rows, part, part_in, half_out, half_in, back, returned, mixed, final,
    load_sem, cache_sem, tab_s, tab_r, gath_s, gath_r, out_s, out_r, fwd_s, fwd_r, back_s, back_r, fin_s, fin_r,
):
    ep, role = lax.axis_index("ep"), lax.axis_index("role")
    z, x = ep // nx, ep % nx
    half = x % 2
    mine = x * 2 + role
    quarter = half * 2 + role
    sibling = {"ep": ep, "role": 1 - role}
    pair = {"ep": ep + 1 - 2 * half, "role": role}
    count, width = out.shape
    qw = packed.shape[-1]
    block = nx * capacity
    offsets, opposite = ring_offsets(nz)
    plane = [(d, f) for d in range(nx) for f in range(2) if d or f]

    def in_plane(d, f):
        other_x, other_role = (x + d) % nx, (role + f) % 2
        return other_x, other_role, {"ep": z * nx + other_x, "role": other_role}

    def place(k):
        return (z + offsets[k] + nz) % nz

    def along_z(k):
        return {"ep": place(k) * nx + x, "role": role}

    def send(src, dst, ssem, rsem, device):
        copy = pltpu.make_async_remote_copy(
            src_ref=src, dst_ref=dst, send_sem=ssem, recv_sem=rsem, device_id=device, device_id_type=MESH
        )
        copy.start()
        return copy

    barrier = pltpu.get_barrier_semaphore()
    for d, f in plane:
        pl.semaphore_signal(barrier, inc=1, device_id=in_plane(d, f)[2], device_id_type=MESH)
    for k in range(nz - 1):
        pl.semaphore_signal(barrier, inc=1, device_id=along_z(k), device_id_type=MESH)

    loads = {}
    for n, (name, src, dst) in enumerate((
        ("queries", queries_hbm, queries_v), ("key_new", key_new_hbm, key_new), ("sink", sink_hbm, sink_v),
        ("ids", ids_hbm, ids_v), ("logits", logits_hbm, logits_v), ("value_new", value_new_hbm, value_new),
        ("residual", residual_hbm, residual_v), ("gain", gain_hbm, gain),
        ("up", up_hbm, up), ("down", down_hbm, down),
    )):
        loads[name] = pltpu.make_async_copy(src, dst, load_sem.at[n])
    cache = [
        [pltpu.make_async_copy(src.at[t], dst.at[t], cache_sem.at[i, t]) for t in range(count)]
        for i, (src, dst) in enumerate(((key_hbm, keys), (value_hbm, values)))
    ]
    for name in ("ids", "logits", "queries", "key_new", "sink"):
        loads[name].start()
    for copies in cache:
        for copy in copies:
            copy.start()
    for name in ("value_new", "residual", "gain", "up", "down"):
        loads[name].start()

    lanes = table.shape[-1]
    experts = table.shape[0] * nz
    lane8 = lax.broadcasted_iota(jnp.int32, (8, lanes), 1)
    lanes_v[...] = jnp.zeros(lanes_v.shape, F32)
    loads["ids"].wait()
    loads["logits"].wait()
    tokens_here = ids_v.shape[1]
    lanes_v[0, :picks, :tokens_here] = ids_v[...].astype(F32)
    lanes_v[1, :picks, :tokens_here] = logits_v[...]
    shift = ROWS - count
    filled = (lane8 % ROWS < count) & (lane8 < 2 * ROWS)

    def to_column(block8):
        return jnp.where(lane8 < ROWS, block8, pltpu.roll(block8, shift, 1))

    chosen = jnp.where(filled, to_column(lanes_v[0]), -1.0)
    logit = to_column(lanes_v[1])
    top = logit[0:1]
    for k in range(1, picks):
        top = jnp.maximum(top, logit[k : k + 1])
    raised = jnp.exp(logit - top)
    total = raised[0:1]
    for k in range(1, picks):
        total = total + raised[k : k + 1]
    gate = raised / total
    chosen = pltpu.roll(chosen, x * 2 * ROWS, 1)
    gate = pltpu.roll(gate, x * 2 * ROWS, 1)
    line = lax.broadcasted_iota(jnp.int32, (experts, lanes), 0)
    expert = ((line % nz) * (nx // 2) + line // nz).astype(F32)
    hits = jnp.zeros((experts, lanes), F32)
    weight = jnp.zeros((experts, lanes), F32)
    for k in range(picks):
        is_it = jnp.broadcast_to(chosen[k : k + 1], (experts, lanes)) == expert
        hits = hits + jnp.where(is_it, 1.0, 0.0)
        weight = weight + jnp.where(is_it, jnp.broadcast_to(gate[k : k + 1], (experts, lanes)), 0.0)
    before = lax.broadcasted_iota(jnp.int32, (lanes, lanes), 0) < lax.broadcasted_iota(jnp.int32, (lanes, lanes), 1)
    earlier = jnp.dot(
        hits.astype(BF16), jnp.where(before, 1.0, 0.0).astype(BF16), preferred_element_type=F32
    )
    table[...] = jnp.where(earlier > 0.5, -weight, weight).astype(BF16).reshape(table.shape)

    kv_width = key_new.shape[1]
    heads_kv = kv_width // HD
    heads = width // HD
    group = heads // heads_kv
    lines = by_group.shape[0]
    low = lax.broadcasted_iota(jnp.int32, (ROWS, 128), 1) < HD

    def half_tile(ref_tile, is_high, want_high):
        return ref_tile if is_high == want_high else pltpu.roll(ref_tile, HD, 1)

    last = width - 3 * qw
    clear = last // 128 * 128
    normed[3, :, clear:] = jnp.zeros((ROWS, qw - clear), BF16)
    part[1, 1, :, :, clear:] = jnp.zeros((nz, block, qw - clear), BF16)
    wide[...] = jnp.zeros(wide.shape, F32)
    by_group[group:] = jnp.zeros((lines - group, *by_group.shape[1:]), F32)
    by_token[count:] = jnp.zeros((ROWS - count, *by_token.shape[1:]), F32)
    loads["queries"].wait()
    wide[:count, :width] = queries_v[...].astype(F32)

    def head_tile(h):
        return wide[:, h // 2 * 128 : h // 2 * 128 + 128]

    for g in range(group):
        for m in range(0, heads_kv, 2):
            first, second = m * group + g, (m + 1) * group + g
            value = half_tile(head_tile(first), first % 2, 0)
            if m + 1 < heads_kv:
                value = jnp.where(low, value, half_tile(head_tile(second), second % 2, 1))
                by_group[g, :, m * HD : m * HD + 128] = value
            else:
                by_group[g, :, m * HD : m * HD + HD] = value[:, :HD]
    loads["sink"].wait()
    lanes_v[0, 0:1, :heads] = sink_v[...]
    row = lax.broadcasted_iota(jnp.int32, (heads_kv * lines, lanes), 0)
    col = lax.broadcasted_iota(jnp.int32, (heads_kv * lines, lanes), 1)
    of_head = (row // lines * group + row % lines == col) & (row % lines < group)
    spread = jnp.broadcast_to(lanes_v[0, 0:1, :], (heads_kv * lines, lanes))
    sink = jnp.sum(jnp.where(of_head, spread, 0.0), axis=1, keepdims=True)
    loads["key_new"].wait()
    loads["value_new"].wait()
    fresh_keys, fresh_values = key_new[...].astype(F32), value_new[...].astype(F32)
    kv_of = lax.broadcasted_iota(jnp.int32, (lines, kv_width), 1) // HD
    window = keys.shape[2]
    slot = lax.broadcasted_iota(jnp.int32, (heads_kv * lines, window), 1)
    scale = HD ** (-0.5)
    for t in range(count):
        query = by_group[:, t, :]
        query = jnp.concatenate([jnp.where(kv_of == k, query, 0.0) for k in range(heads_kv)], axis=0)
        cache[0][t].wait()
        cached = jnp.dot(query.astype(BF16), keys[t], preferred_element_type=F32) * scale
        fresh = jnp.sum(query * fresh_keys[t : t + 1], axis=1, keepdims=True) * scale
        length = lengths[t]
        newest = length - 1
        position = newest - jnp.bitwise_and(newest - slot, window - 1)
        visible = (position >= 0) & (position >= length - window + 1)
        cached = jnp.where(visible, cached, -1e30)
        highest = jnp.maximum(jnp.maximum(jnp.max(cached, axis=1, keepdims=True), fresh), sink)
        weights = jnp.exp(cached - highest)
        fresh_weight = jnp.exp(fresh - highest)
        denominator = jnp.sum(weights, axis=1, keepdims=True) + fresh_weight + jnp.exp(sink - highest)
        probs = (weights / denominator).astype(BF16)
        fresh_prob = (fresh_weight / denominator).astype(BF16).astype(F32)
        cache[1][t].wait()
        seen = lax.dot_general(probs, values[t], (((1,), (1,)), ((), ())), preferred_element_type=F32)
        seen = seen + fresh_prob * fresh_values[t : t + 1]
        merged = None
        for k in range(heads_kv):
            term = jnp.where(kv_of == k, seen[k * lines : (k + 1) * lines], 0.0)
            merged = term if merged is None else merged + term
        by_token[t, :, :kv_width] = merged
    loads["residual"].wait()
    wide[:count, :width] = residual_v[...].astype(F32)

    def context_tile(h, want_high):
        g, k = h % group, h // group
        return half_tile(by_token[:, g, k // 2 * 128 : k // 2 * 128 + 128], k % 2, want_high)

    for j in range(wide.shape[1] // 128):
        upper = context_tile(2 * j + 1, 1) if 2 * j + 1 < heads else 0.0
        hidden[:, j * 128 : (j + 1) * 128] = wide[:, j * 128 : (j + 1) * 128] + jnp.where(
            low, context_tile(2 * j, 0), upper
        )
    state = hidden[:, :width]
    inverse = lax.rsqrt(jnp.sum(state * state, axis=1, keepdims=True) * (1.0 / width) + 1e-05)
    loads["gain"].wait()
    for q in range(4):
        w = min(qw, width - q * qw)
        cut = slice(q * qw, q * qw + w)
        normed[q, :, :w] = (hidden[:, cut] * inverse * gain[:, cut]).astype(BF16)

    pl.semaphore_wait(barrier, len(plane) + nz - 1)

    tab_copies, gath_copies = [], []
    for n, (d, f) in enumerate(plane):
        other_x, other_role, device = in_plane(d, f)
        if f == 0:
            tab_copies.append(send(table.at[other_x // 2], tabs.at[x], tab_s.at[d], tab_r.at[d], device))
        wanted = (other_x % 2) * 2 + other_role
        gath_copies.append(send(normed.at[wanted], gath.at[mine], gath_s.at[n], gath_r.at[n], device))
    gath[mine] = normed[quarter]
    tabs[x] = table[x // 2]
    for copy in tab_copies:
        copy.wait_recv()
    codes = jnp.sum(tabs[...].astype(F32), axis=0)
    row = lax.broadcasted_iota(jnp.int32, (nz, block, lanes), 1)
    col = lax.broadcasted_iota(jnp.int32, (nz, block, lanes), 2)
    codes = jnp.broadcast_to(codes[:, None, :], (nz, block, lanes))
    signed = jnp.where(row % capacity == 0, codes, -codes)
    hit = (col // (2 * ROWS) == row // capacity) & (signed > 0.0)
    choose = jnp.where(hit, 1.0, 0.0).astype(BF16).reshape(nz * block, lanes)
    blend = jnp.where(hit, signed, 0.0).astype(BF16).reshape(nz * block, lanes)
    for copy in gath_copies:
        copy.wait_recv()
    tokens = gath[...].reshape(2 * nx * ROWS, qw)
    if tokens.shape[0] < lanes:
        tokens = jnp.concatenate([tokens, jnp.zeros((lanes - tokens.shape[0], qw), BF16)], axis=0)
    packed[...] = jnp.dot(choose, tokens, preferred_element_type=F32).astype(BF16).reshape(nz, block, qw)

    out_copies = {}
    for k in range(nz - 1):
        to = opposite[k]
        out_copies[k] = send(packed.at[place(k)], rows.at[quarter, to], out_s.at[k], out_r.at[to], along_z(k))
    rows[quarter, nz - 1] = packed[z]
    back_copies = {}
    live = {}
    starts = [sum(chunks[:c]) for c in range(len(chunks))]

    def span(c):
        return pl.ds(starts[c], chunks[c])

    def blocks(c):
        return range(starts[c], starts[c] + chunks[c])

    def stage_in(c):
        for k in blocks(c):
            if k < nz - 1:
                out_copies[opposite[k]].wait_recv()
            one = rows.at[quarter, k]
            live["pair", k] = send(one, one, fwd_s.at[0, k], fwd_r.at[0, k], pair)
        mine_rows = rows.at[quarter, span(c)]
        live["sib", c] = send(mine_rows, mine_rows, fwd_s.at[1, c], fwd_r.at[1, c], sibling)

    def stage_relay(c):
        for k in blocks(c):
            live["pair", k].wait_recv()
        their_rows = rows.at[(1 - half) * 2 + role, span(c)]
        live["relay", c] = send(their_rows, their_rows, fwd_s.at[2, c], fwd_r.at[2, c], sibling)

    def stage_ffn(c):
        live["sib", c].wait_recv()
        live["relay", c].wait_recv()
        if c == 0:
            loads["up"].wait()
        at = slice(starts[c], starts[c] + chunks[c])
        total = None
        for q in range(4):
            w = min(qw, width - q * qw)
            piece = rows[q, at, :, :w].reshape(chunks[c] * block, w)
            term = lax.dot_general(
                piece, up[:, q * qw : q * qw + w], (((1,), (1,)), ((), ())), preferred_element_type=F32
            )
            total = term if total is None else total + term
        active = (total / (1.0 + jnp.exp(-total))).astype(BF16)
        if c == 0:
            loads["down"].wait()
        for q in range(4):
            w = min(qw, width - q * qw)
            value = jnp.dot(active, down[:, q * qw : q * qw + w], preferred_element_type=F32).astype(BF16)
            part[q // 2, q % 2, at, :, :w] = value.reshape(chunks[c], block, w)
        live["part", c] = send(
            part.at[:, 1 - role, span(c)], part_in.at[:, span(c)], fwd_s.at[3, c], fwd_r.at[3, c], sibling
        )

    def stage_half(c):
        live["part", c].wait_recv()
        at = slice(starts[c], starts[c] + chunks[c])
        half_out[at] = (part[1 - half, role, at].astype(F32) + part_in[1 - half, at].astype(F32)).astype(BF16)
        for k in blocks(c):
            live["half", k] = send(half_out.at[k], half_in.at[k], fwd_s.at[4, k], fwd_r.at[4, k], pair)

    def stage_back(c):
        for k in blocks(c):
            live["half", k].wait_recv()
            back[k] = (
                part[half, role, k].astype(F32) + part_in[half, k].astype(F32) + half_in[k].astype(F32)
            ).astype(BF16)
            if k == nz - 1:
                returned[z] = back[k]
            else:
                back_copies[k] = send(
                    back.at[k], returned.at[z], back_s.at[k], back_r.at[opposite[k]], along_z(k)
                )

    stages = {"i": stage_in, "r": stage_relay, "f": stage_ffn, "h": stage_half, "b": stage_back}
    for step in order.split():
        stages[step[0]](int(step[1:]))

    for k in range(nz - 1):
        back_copies[opposite[k]].wait_recv()
    mix = lax.dot_general(
        blend, returned[...].reshape(nz * block, qw), (((0,), (0,)), ((), ())), preferred_element_type=F32
    )
    mixed[...] = mix[: 2 * nx * ROWS].astype(BF16).reshape(2 * nx, ROWS, qw)
    fin_copies = []
    for n, (d, f) in enumerate(plane):
        other_x, other_role, device = in_plane(d, f)
        fin_copies.append(
            send(mixed.at[other_x * 2 + other_role], final.at[mine], fin_s.at[n], fin_r.at[n], device)
        )
    final[mine] = mixed[mine]
    for copy in fin_copies:
        copy.wait_recv()
    for q in range(4):
        total = None
        for p in range(nx // 2):
            term = final[(2 * p + q // 2) * 2 + q % 2].astype(F32)
            total = term if total is None else total + term
        w = min(qw, width - q * qw)
        cut = slice(q * qw, q * qw + w)
        out[:, cut] = (hidden[:count, cut] + total[:count, :w]).astype(BF16)
    for copy in (
        tab_copies + gath_copies + list(out_copies.values()) + list(live.values())
        + list(back_copies.values()) + fin_copies
    ):
        copy.wait_send()


def local(
    residual,
    queries,
    key_new,
    value_new,
    key_cache,
    value_cache,
    lengths,
    sink_logits,
    norm_gain,
    route_ids,
    route_logits,
    up_weight,
    down_weight,
):
    pair_count, picks = route_ids.shape
    rank_count = lax.axis_size("ep")
    experts = rank_count // 2
    capacity = min(pair_count, max(2, (pair_count * picks + experts - 1) // experts))
    nx = TILE // capacity
    nz = rank_count // nx
    count, width = residual.shape
    window, kv_width = key_cache.shape[1:]
    heads_kv = kv_width // HD
    group = width // kv_width
    lines = -(-group // 16) * 16
    hidden_units = up_weight.shape[1]
    qw = -(-width // (4 * 128)) * 128
    padded = -(-width // 128) * 128
    lanes = 128
    block = nx * capacity
    chunks = CHUNKS if sum(CHUNKS) == nz else [nz]
    order = ORDER if sum(CHUNKS) == nz else "i0 r0 f0 h0 b0"
    dma = pltpu.SemaphoreType.DMA
    any_space = pl.BlockSpec(memory_space=pl.ANY)

    def vmem(*shape, dtype=BF16):
        return pltpu.VMEM(shape, dtype)

    return pl.pallas_call(
        functools.partial(layer_kernel, nx, nz, capacity, picks, chunks, order),
        out_shape=jax.ShapeDtypeStruct((count, width), BF16),
        in_specs=[pl.BlockSpec(memory_space=pltpu.SMEM)] + [any_space] * 12,
        out_specs=pl.BlockSpec(memory_space=pltpu.VMEM),
        scratch_shapes=[
            vmem(count, width),
            vmem(count, width),
            vmem(count, kv_width),
            vmem(count, kv_width),
            vmem(count, kv_width, window),
            vmem(count, kv_width, window),
            vmem(1, sink_logits.shape[0], dtype=F32),
            vmem(1, width, dtype=F32),
            vmem(picks, pair_count, dtype=jnp.int32),
            vmem(picks, pair_count, dtype=F32),
            vmem(ROWS, padded, dtype=F32),
            vmem(lines, ROWS, kv_width, dtype=F32),
            vmem(ROWS, lines, -(-kv_width // 128) * 128, dtype=F32),
            vmem(ROWS, padded, dtype=F32),
            vmem(2, 8, lanes, dtype=F32),
            vmem(4, ROWS, qw),
            vmem(nx // 2, nz, lanes),
            vmem(hidden_units, width),
            vmem(hidden_units, width),
            vmem(2 * nx, ROWS, qw),
            vmem(nx, nz, lanes),
            vmem(nz, block, qw),
            vmem(4, nz, block, qw),
            vmem(2, 2, nz, block, qw),
            vmem(2, nz, block, qw),
            vmem(nz, block, qw),
            vmem(nz, block, qw),
            vmem(nz, block, qw),
            vmem(nz, block, qw),
            vmem(2 * nx, ROWS, qw),
            vmem(2 * nx, ROWS, qw),
            dma((10,)),
            dma((2, count)),
            dma((nx,)), dma((nx,)),
            dma((2 * nx,)), dma((2 * nx,)),
            dma((nz,)), dma((nz,)),
            dma((5, nz)), dma((5, nz)),
            dma((nz,)), dma((nz,)),
            dma((2 * nx,)), dma((2 * nx,)),
        ],
        compiler_params=pltpu.CompilerParams(collective_id=0, has_side_effects=True),
        name="layer",
    )(
        lengths, residual, queries, key_new, value_new,
        key_cache.transpose(0, 2, 1), value_cache.transpose(0, 2, 1),
        sink_logits.reshape(1, -1), norm_gain.reshape(1, -1), route_ids.T, route_logits.T,
        up_weight.T, down_weight,
    )


def solution(mesh):
    placed = (
        P(("groups", "ep", "role"), None),
        P(("groups", "ep", "role"), None),
        P(("groups", "ep", "role"), None),
        P(("groups", "ep", "role"), None),
        P(("groups", "ep", "role"), None, None),
        P(("groups", "ep", "role"), None, None),
        P(("groups", "ep", "role")),
        P(),
        P(),
        P(("groups", "ep"), None),
        P(("groups", "ep"), None),
        P(None, ("ep", "role")),
        P(("ep", "role"), None),
    )
    return jax.shard_map(
        local,
        mesh=mesh,
        in_specs=placed,
        out_specs=P(("groups", "ep", "role"), None),
        check_vma=False,
    )
```

time: 132 us -> 118 us (0.89)
  local copies, waits for them, and re-layouts: 8.68 us -> 2.73 us
  other arithmetic: 5.85 us -> 0 us
  matrix products: 2.77 us -> 0 us
  Pallas kernels: 114 us -> 116 us
    unnamed x10 -> x1, local copies, waits for them, and re-layouts: 4.38 us -> 1.42 us
    dot_general x4 -> x0, matrix products: 2.77 us -> none  [the longest x1 1.45 us: attention(): jnp.einsum('tkgs,tskd->tkgd', cache_probs, cached_values, preferred_eleme...]
    pallas_call x1, Pallas kernels: 114 us -> 116 us  [local(): pl.pallas_call(functools.partial(layer_kernel, nx, nz, capacity, picks, c...]
    convert_element_type x3 -> x0, other arithmetic: 1.64 us -> none  [the longest x1 1.53 us: local(): return (hidden_state + expert_out[:count, :width]).astype(BF16)]
where the time goes in v2:
time: 118 us
  Pallas kernels  116 us (98%)
  local copies, waits for them, and re-layouts  2.73 us (2%)
    pallas_call x1, Pallas kernels, local(): pl.pallas_call(functools.partial(layer_kernel, nx, nz, capacity, picks, c...  116 us

profile of v2, /device:TPU:65, one launch (start us, length us, event | category | flops | bytes accessed | tf_op | source)
XLA Modules:
  0.0 118.3 jit_solution(5541884191395151231)
XLA Ops:
  0.0 1.3 %reshape.7.gain_hbm = f32[1,2880]{1,0:T(1,128)} reshape(f32[2880]{0:T(1024)} %param.21) | data formatting | bytes 23040 | tf_op jit(solution)/shard_map/reshape | solution.py:453
  1.3 115.5 %layer.1 = bf16[6,2880]{1,0:T(8,128)(2,1)} custom-call(s32[6]{0:T(128)} %lengths.1, bf16[6,2880]{1,0:T(8,128)(2,1)} %residual_hbm.1, bf16[6,2880]{1,0:T(8,128)(2,1)} %queries_hbm.1, bf16[6,320]{1,0:T(8,128)(2,1)} %key_new_hbm.1, bf16[6,320]{1,0:T(8,128)(2,1)} %value_new_hbm.1, bf16[6,320,128]{2,1,0:T(8,128)(2,1)} %bitcast.7, bf16[6,320,128]{2,1,0:T(8,128)(2,1)} %bitcast.8, ...), custom_call_target="tpu_custom_call" | custom-call | tf_op jit(solution)/shard_map/layer/pallas_call | solution.py:402
  116.8 1.4 %copy.15 = bf16[6,2880]{1,0:T(8,128)(2,1)} copy(bf16[6,2880]{1,0:T(8,128)(2,1)} %layer.1) | data formatting | bytes 69120

commit v3 on v2

--- a/solution.py
+++ b/solution.py
@@ -10,8 +10,8 @@
 HD = 64
 ROWS = 8
 TILE = 16
-ORDER = "i0 r0 f0 i1 h0 r1 f1 b0 i2 h1 r2 f2 b1 i3 h2 r3 f3 b2 h3 b3"
-CHUNKS = [4, 4, 4, 4]
+ORDER = ("i0 r0 i1 f0", "i2 h0 r1 f1", "b0 h1 i3 r2", "f2 b1 r3 h2", "f3 b2 h3 b3")
+CHUNKS = [2, 3, 5, 6]
 MESH = pl.DeviceIdType.MESH
 BF16 = jnp.bfloat16
 F32 = jnp.float32
@@ -32,7 +32,7 @@
     ids_hbm, logits_hbm, up_hbm, down_hbm, out,
     residual_v, queries_v, key_new, value_new, keys, values, sink_v, gain, ids_v, logits_v,
     wide, by_group, by_token, hidden, lanes_v, normed, table,
-    up, down, gath, tabs, packed, rows, part, part_in, half_out, half_in, back, returned, mixed, final,
+    up, down, up4, down4, gath, tabs, packed, rows, part, part_in, half_out, half_in, back, returned, mixed, final,
     load_sem, cache_sem, tab_s, tab_r, gath_s, gath_r, out_s, out_r, fwd_s, fwd_r, back_s, back_r, fin_s, fin_r,
 ):
     ep, role = lax.axis_index("ep"), lax.axis_index("role")
@@ -83,20 +83,27 @@
         [pltpu.make_async_copy(src.at[t], dst.at[t], cache_sem.at[i, t]) for t in range(count)]
         for i, (src, dst) in enumerate(((key_hbm, keys), (value_hbm, values)))
     ]
-    for name in ("ids", "logits", "queries", "key_new", "sink"):
+    early = ("queries", "ids", "logits", "key_new", "sink", "value_new", "residual", "gain")
+    for name in early:
         loads[name].start()
     for copies in cache:
         for copy in copies:
             copy.start()
-    for name in ("value_new", "residual", "gain", "up", "down"):
+    for name in ("up", "down"):
         loads[name].start()
 
     lanes = table.shape[-1]
     experts = table.shape[0] * nz
     lane8 = lax.broadcasted_iota(jnp.int32, (8, lanes), 1)
     lanes_v[...] = jnp.zeros(lanes_v.shape, F32)
-    loads["ids"].wait()
-    loads["logits"].wait()
+    normed[3] = jnp.zeros((ROWS, qw), BF16)
+    wide[...] = jnp.zeros(wide.shape, F32)
+    heads_kv = key_new.shape[1] // HD
+    group = width // HD // heads_kv
+    by_group[group:] = jnp.zeros((by_group.shape[0] - group, *by_group.shape[1:]), F32)
+    by_token[count:] = jnp.zeros((ROWS - count, *by_token.shape[1:]), F32)
+    for name in early:
+        loads[name].wait()
     tokens_here = ids_v.shape[1]
     lanes_v[0, :picks, :tokens_here] = ids_v[...].astype(F32)
     lanes_v[1, :picks, :tokens_here] = logits_v[...]
@@ -133,23 +140,13 @@
     table[...] = jnp.where(earlier > 0.5, -weight, weight).astype(BF16).reshape(table.shape)
 
     kv_width = key_new.shape[1]
-    heads_kv = kv_width // HD
     heads = width // HD
-    group = heads // heads_kv
     lines = by_group.shape[0]
     low = lax.broadcasted_iota(jnp.int32, (ROWS, 128), 1) < HD
 
     def half_tile(ref_tile, is_high, want_high):
         return ref_tile if is_high == want_high else pltpu.roll(ref_tile, HD, 1)
 
-    last = width - 3 * qw
-    clear = last // 128 * 128
-    normed[3, :, clear:] = jnp.zeros((ROWS, qw - clear), BF16)
-    part[1, 1, :, :, clear:] = jnp.zeros((nz, block, qw - clear), BF16)
-    wide[...] = jnp.zeros(wide.shape, F32)
-    by_group[group:] = jnp.zeros((lines - group, *by_group.shape[1:]), F32)
-    by_token[count:] = jnp.zeros((ROWS - count, *by_token.shape[1:]), F32)
-    loads["queries"].wait()
     wide[:count, :width] = queries_v[...].astype(F32)
 
     def head_tile(h):
@@ -164,46 +161,48 @@
                 by_group[g, :, m * HD : m * HD + 128] = value
             else:
                 by_group[g, :, m * HD : m * HD + HD] = value[:, :HD]
-    loads["sink"].wait()
     lanes_v[0, 0:1, :heads] = sink_v[...]
     row = lax.broadcasted_iota(jnp.int32, (heads_kv * lines, lanes), 0)
     col = lax.broadcasted_iota(jnp.int32, (heads_kv * lines, lanes), 1)
     of_head = (row // lines * group + row % lines == col) & (row % lines < group)
     spread = jnp.broadcast_to(lanes_v[0, 0:1, :], (heads_kv * lines, lanes))
     sink = jnp.sum(jnp.where(of_head, spread, 0.0), axis=1, keepdims=True)
-    loads["key_new"].wait()
-    loads["value_new"].wait()
     fresh_keys, fresh_values = key_new[...].astype(F32), value_new[...].astype(F32)
     kv_of = lax.broadcasted_iota(jnp.int32, (lines, kv_width), 1) // HD
     window = keys.shape[2]
     slot = lax.broadcasted_iota(jnp.int32, (heads_kv * lines, window), 1)
     scale = HD ** (-0.5)
+    for copy in cache[0]:
+        copy.wait()
+    scores, fresh_scores, seen = [], [], []
     for t in range(count):
         query = by_group[:, t, :]
         query = jnp.concatenate([jnp.where(kv_of == k, query, 0.0) for k in range(heads_kv)], axis=0)
-        cache[0][t].wait()
-        cached = jnp.dot(query.astype(BF16), keys[t], preferred_element_type=F32) * scale
-        fresh = jnp.sum(query * fresh_keys[t : t + 1], axis=1, keepdims=True) * scale
+        scores.append(jnp.dot(query.astype(BF16), keys[t], preferred_element_type=F32) * scale)
+        fresh_scores.append(jnp.sum(query * fresh_keys[t : t + 1], axis=1, keepdims=True) * scale)
+    for copy in cache[1]:
+        copy.wait()
+    for t in range(count):
+        fresh = fresh_scores[t]
         length = lengths[t]
         newest = length - 1
         position = newest - jnp.bitwise_and(newest - slot, window - 1)
         visible = (position >= 0) & (position >= length - window + 1)
-        cached = jnp.where(visible, cached, -1e30)
+        cached = jnp.where(visible, scores[t], -1e30)
         highest = jnp.maximum(jnp.maximum(jnp.max(cached, axis=1, keepdims=True), fresh), sink)
         weights = jnp.exp(cached - highest)
         fresh_weight = jnp.exp(fresh - highest)
         denominator = jnp.sum(weights, axis=1, keepdims=True) + fresh_weight + jnp.exp(sink - highest)
         probs = (weights / denominator).astype(BF16)
         fresh_prob = (fresh_weight / denominator).astype(BF16).astype(F32)
-        cache[1][t].wait()
-        seen = lax.dot_general(probs, values[t], (((1,), (1,)), ((), ())), preferred_element_type=F32)
-        seen = seen + fresh_prob * fresh_values[t : t + 1]
+        out_t = lax.dot_general(probs, values[t], (((1,), (1,)), ((), ())), preferred_element_type=F32)
+        seen.append(out_t + fresh_prob * fresh_values[t : t + 1])
+    for t in range(count):
         merged = None
         for k in range(heads_kv):
-            term = jnp.where(kv_of == k, seen[k * lines : (k + 1) * lines], 0.0)
+            term = jnp.where(kv_of == k, seen[t][k * lines : (k + 1) * lines], 0.0)
             merged = term if merged is None else merged + term
         by_token[t, :, :kv_width] = merged
-    loads["residual"].wait()
     wide[:count, :width] = residual_v[...].astype(F32)
 
     def context_tile(h, want_high):
@@ -217,7 +216,6 @@
         )
     state = hidden[:, :width]
     inverse = lax.rsqrt(jnp.sum(state * state, axis=1, keepdims=True) * (1.0 / width) + 1e-05)
-    loads["gain"].wait()
     for q in range(4):
         w = min(qw, width - q * qw)
         cut = slice(q * qw, q * qw + w)
@@ -234,6 +232,14 @@
         gath_copies.append(send(normed.at[wanted], gath.at[mine], gath_s.at[n], gath_r.at[n], device))
     gath[mine] = normed[quarter]
     tabs[x] = table[x // 2]
+    loads["up"].wait()
+    loads["down"].wait()
+    for stored, whole in ((up4, up), (down4, down)):
+        for q in range(4):
+            w = min(qw, width - q * qw)
+            if w < qw:
+                stored[q, :, w // 128 * 128 :] = jnp.zeros((whole.shape[0], qw - w // 128 * 128), BF16)
+            stored[q, :, :w] = whole[:, q * qw : q * qw + w]
     for copy in tab_copies:
         copy.wait_recv()
     codes = jnp.sum(tabs[...].astype(F32), axis=0)
@@ -257,7 +263,7 @@
         out_copies[k] = send(packed.at[place(k)], rows.at[quarter, to], out_s.at[k], out_r.at[to], along_z(k))
     rows[quarter, nz - 1] = packed[z]
     back_copies = {}
-    live = {}
+    live, totals = {}, {}
     starts = [sum(chunks[:c]) for c in range(len(chunks))]
 
     def span(c):
@@ -265,6 +271,10 @@
 
     def blocks(c):
         return range(starts[c], starts[c] + chunks[c])
+
+    def up_dot(c, q):
+        piece = rows[q, slice(starts[c], starts[c] + chunks[c])].reshape(chunks[c] * block, qw)
+        return lax.dot_general(piece, up4[q], (((1,), (1,)), ((), ())), preferred_element_type=F32)
 
     def stage_in(c):
         for k in blocks(c):
@@ -274,37 +284,29 @@
             live["pair", k] = send(one, one, fwd_s.at[0, k], fwd_r.at[0, k], pair)
         mine_rows = rows.at[quarter, span(c)]
         live["sib", c] = send(mine_rows, mine_rows, fwd_s.at[1, c], fwd_r.at[1, c], sibling)
+        totals[c] = up_dot(c, quarter)
 
     def stage_relay(c):
         for k in blocks(c):
             live["pair", k].wait_recv()
         their_rows = rows.at[(1 - half) * 2 + role, span(c)]
         live["relay", c] = send(their_rows, their_rows, fwd_s.at[2, c], fwd_r.at[2, c], sibling)
+        live["sib", c].wait_recv()
+        totals[c] = totals[c] + up_dot(c, half * 2 + 1 - role) + up_dot(c, (1 - half) * 2 + role)
 
     def stage_ffn(c):
-        live["sib", c].wait_recv()
         live["relay", c].wait_recv()
-        if c == 0:
-            loads["up"].wait()
         at = slice(starts[c], starts[c] + chunks[c])
-        total = None
-        for q in range(4):
-            w = min(qw, width - q * qw)
-            piece = rows[q, at, :, :w].reshape(chunks[c] * block, w)
-            term = lax.dot_general(
-                piece, up[:, q * qw : q * qw + w], (((1,), (1,)), ((), ())), preferred_element_type=F32
-            )
-            total = term if total is None else total + term
+        total = totals[c] + up_dot(c, (1 - half) * 2 + 1 - role)
         active = (total / (1.0 + jnp.exp(-total))).astype(BF16)
-        if c == 0:
-            loads["down"].wait()
-        for q in range(4):
-            w = min(qw, width - q * qw)
-            value = jnp.dot(active, down[:, q * qw : q * qw + w], preferred_element_type=F32).astype(BF16)
-            part[q // 2, q % 2, at, :, :w] = value.reshape(chunks[c], block, w)
-        live["part", c] = send(
-            part.at[:, 1 - role, span(c)], part_in.at[:, span(c)], fwd_s.at[3, c], fwd_r.at[3, c], sibling
-        )
+        for r in (1 - role, role):
+            for h in range(2):
+                value = jnp.dot(active, down4[h * 2 + r], preferred_element_type=F32).astype(BF16)
+                part[h, r, at] = value.reshape(chunks[c], block, qw)
+            if r is not role:
+                live["part", c] = send(
+                    part.at[:, 1 - role, span(c)], part_in.at[:, span(c)], fwd_s.at[3, c], fwd_r.at[3, c], sibling
+                )
 
     def stage_half(c):
         live["part", c].wait_recv()
@@ -327,7 +329,7 @@
                 )
 
     stages = {"i": stage_in, "r": stage_relay, "f": stage_ffn, "h": stage_half, "b": stage_back}
-    for step in order.split():
+    for step in " ".join(order).split():
         stages[step[0]](int(step[1:]))
 
     for k in range(nz - 1):
@@ -392,7 +394,7 @@
     lanes = 128
     block = nx * capacity
     chunks = CHUNKS if sum(CHUNKS) == nz else [nz]
-    order = ORDER if sum(CHUNKS) == nz else "i0 r0 f0 h0 b0"
+    order = ORDER if sum(CHUNKS) == nz else ("i0 r0 f0", "h0 b0")
     dma = pltpu.SemaphoreType.DMA
     any_space = pl.BlockSpec(memory_space=pl.ANY)
 
@@ -424,6 +426,8 @@
             vmem(nx // 2, nz, lanes),
             vmem(hidden_units, width),
             vmem(hidden_units, width),
+            vmem(4, hidden_units, qw),
+            vmem(4, hidden_units, qw),
             vmem(2 * nx, ROWS, qw),
             vmem(nx, nz, lanes),
             vmem(nz, block, qw),

time: 118 us -> 115 us (0.975)
  Pallas kernels: 116 us -> 112 us
    pallas_call x1, Pallas kernels: 116 us -> 112 us  [local(): pl.pallas_call(functools.partial(layer_kernel, nx, nz, capacity, picks, c...]
where the time goes in v3:
time: 115 us
  Pallas kernels  112 us (97%)
  local copies, waits for them, and re-layouts  2.73 us (2%)
    pallas_call x1, Pallas kernels, local(): pl.pallas_call(functools.partial(layer_kernel, nx, nz, capacity, picks, c...  112 us

profile of v3, /device:TPU:65, one launch (start us, length us, event | category | flops | bytes accessed | tf_op | source)
XLA Modules:
  0.0 114.9 jit_solution(13628720096864807975)
XLA Ops:
  0.0 1.3 %reshape.7.gain_hbm = f32[1,2880]{1,0:T(1,128)} reshape(f32[2880]{0:T(1024)} %param.21) | data formatting | bytes 23040 | tf_op jit(solution)/shard_map/reshape | solution.py:457
  1.3 112.1 %layer.1 = bf16[6,2880]{1,0:T(8,128)(2,1)} custom-call(s32[6]{0:T(128)} %lengths.1, bf16[6,2880]{1,0:T(8,128)(2,1)} %residual_hbm.1, bf16[6,2880]{1,0:T(8,128)(2,1)} %queries_hbm.1, bf16[6,320]{1,0:T(8,128)(2,1)} %key_new_hbm.1, bf16[6,320]{1,0:T(8,128)(2,1)} %value_new_hbm.1, bf16[6,320,128]{2,1,0:T(8,128)(2,1)} %bitcast.7, bf16[6,320,128]{2,1,0:T(8,128)(2,1)} %bitcast.8, ...), custom_call_target="tpu_custom_call" | custom-call | tf_op jit(solution)/shard_map/layer/pallas_call | solution.py:404
  113.5 1.4 %copy.15 = bf16[6,2880]{1,0:T(8,128)(2,1)} copy(bf16[6,2880]{1,0:T(8,128)(2,1)} %layer.1) | data formatting | bytes 69120
